TPU v7x, 512 devices: a whole 4x8x8 slice. The times are simulated.
512 devices in a mesh: row: 32 (over y_lo, x, core), col: 16 (over z, y_hi).
Axes of the slice: x: 4, y: 8 (y_hi: 2, y_lo: 4; y = y_hi * 4 + y_lo), z: 8, core: 2. Of those that a mesh axis runs over, the one named last changes fastest.
Arguments:
- left_act: bfloat16 [32, 64, 1024], P(None, 'col', 'row'), may hold values from -6 to 6
- right_act: bfloat16 [32, 64, 1024], P(None, 'row', 'col'), may hold values from -6 to 6
- cotangent: bfloat16 [1024, 1024, 128], P('row', 'col'), may hold values from -4 to 4
- weight: bfloat16 [1024, 128], replicated, may hold values from -0.1875 to 0.1875
Outputs:
- grad_left: float32 [32, 64, 1024], P(None, 'col', 'row')
- grad_right: float32 [32, 64, 1024], P(None, 'row', 'col')
- grad_weight: float32 [1024, 128], P('row')
All inputs are finite; a program needn't handle non-finite values.
Results may differ from a plain program's by a relative error of at most 0.0029.
Values may be sent and summed in bfloat16 or wider, within the bound.
A program may use at most 128 MiB of HBM per device.

v0:
```python
import jax
import jax.numpy as jnp
from jax import lax
from jax.sharding import PartitionSpec as P

S = 64


def sent_to_all(shard, axis):
    count = lax.axis_size(axis)
    return lax.all_to_all(
        jnp.broadcast_to(shard[None], (count, *shard.shape)), axis, 0, 0, tiled=True
    )


def laid_out(tiles, dim):
    lengths = list(tiles.shape[1:])
    lengths[dim] *= tiles.shape[0]
    return jnp.moveaxis(tiles, 0, dim).reshape(lengths)


def gathered_copies(shard, axis, dim):
    tiles = sent_to_all(shard, axis)
    return laid_out(tiles, dim)


def in_blocks(shard, dim, count):
    lengths = shard.shape
    tiles = shard.reshape(*lengths[:dim], count, lengths[dim] // count, *lengths[dim + 1 :])
    return jnp.moveaxis(tiles, dim, 0)


def summed_on_arrival(shard, axis, dim):
    count = lax.axis_size(axis)
    tiles = lax.all_to_all(in_blocks(shard, dim, count), axis, 0, 0, tiled=True)
    return jnp.sum(tiles, axis=0)


def of_everyone(shard, axis):
    return sent_to_all(shard, axis).sum(axis=0)


def body(left_act, right_act, cotangent, weight):
    left = gathered_copies(left_act, "col", 1)
    right = gathered_copies(right_act, "row", 1)
    first, second = (cotangent.shape[0], cotangent.shape[1])
    chans = left.shape[0]
    outer = (
        jnp.einsum("csi,dsj->ijcd", left, right, preferred_element_type=jnp.float32) / S
    ).astype(jnp.bfloat16)
    outer_flat = outer.reshape(first * second, chans * chans)
    grad_flat = cotangent.reshape(first * second, cotangent.shape[2])
    contract = (((0,), (0,)), ((), ()))
    partial_w = lax.dot_general(outer_flat, grad_flat, contract, preferred_element_type=jnp.float32)
    own_rows = summed_on_arrival(partial_w, "row", 0)
    grad_weight = of_everyone(own_rows, "col")
    grad_outer = lax.dot_general(
        grad_flat, weight, (((1,), (1,)), ((), ())), preferred_element_type=jnp.float32
    )
    grad_outer = grad_outer.astype(jnp.bfloat16).reshape(first, second, chans, chans)
    left_part = (
        jnp.einsum("ijcd,dsj->csi", grad_outer, right, preferred_element_type=jnp.float32) / S
    )
    right_part = (
        jnp.einsum("ijcd,csi->dsj", grad_outer, left, preferred_element_type=jnp.float32) / S
    )
    grad_left = summed_on_arrival(left_part, "col", 1)
    grad_right = summed_on_arrival(right_part, "row", 1)
    return (grad_left, grad_right, grad_weight)


def solution(mesh):
    return jax.shard_map(
        body,
        mesh=mesh,
        in_specs=(P(None, "col", "row"), P(None, "row", "col"), P("row", "col", None), P()),
        out_specs=(P(None, "col", "row"), P(None, "row", "col"), P("row", None)),
        check_vma=False,
    )
```

profile of v0, /device:TPU:8, one launch (start us, length us, event | category | flops | bytes accessed | tf_op | source)
XLA Modules:
  0.0 178.2 jit_solution(4026763738388362372)
XLA Ops:
  0.6 0.8 copy.32
  1.6 1.2 reshape.49
  2.7 14.8 %all-to-all-start.2 = ((bf16[16,2,2048]{2,1,0:T(2,128)(2,1)}), bf16[16,2,2048]{2,1,0:T(2,128)(2,1)S(1)}, u32[]{:S(2)}, u32[]{:S(2)}) async-start(bf16[16,2,2048]{2,1,0:T(2,128)(2,1)} %reshape.49), calls=%async_computation.2 | async-start | bytes 262144 | tf_op jit(solution)/shard_map/all_to_all | solution.py:11
  17.5 1.2 broadcast_in_dim.6
  18.7 1.1 reshape.45
  19.8 11.2 %all-to-all-done.2 = bf16[16,2,2048]{2,1,0:T(2,128)(2,1)S(1)} async-done(((bf16[16,2,2048]{2,1,0:T(2,128)(2,1)}), bf16[16,2,2048]{2,1,0:T(2,128)(2,1)S(1)}, u32[]{:S(2)}, u32[]{:S(2)}) %all-to-all-start.2) | async-done | bytes 131104 | tf_op jit(solution)/shard_map/all_to_all | solution.py:11
  31.0 6.1 %all-to-all-start = ((bf16[32,2,2048]{2,1,0:T(2,128)(2,1)}), bf16[32,2,2048]{2,1,0:T(2,128)(2,1)S(1)}, u32[]{:S(2)}, u32[]{:S(2)}) async-start(bf16[32,2,2048]{2,1,0:T(2,128)(2,1)} %reshape.45), calls=%async_computation | async-start | bytes 524288 | tf_op jit(solution)/shard_map/all_to_all | solution.py:11
  37.1 4.1 %convolution_convert_fusion = bf16[2048,1024]{1,0:T(8,128)(2,1)} fusion(bf16[2048,128]{1,0:T(8,128)(2,1)S(1)} %bitcast.68, bf16[1024,128]{1,0:T(8,128)(2,1)} %param.7), kind=kOutput, calls=%fused_computation.2 | convolution fusion | flops 538968064 | bytes 4980736 | tf_op jit(solution)/shard_map/dot_general | solution.py:57
  41.2 6.5 %copy.29 = bf16[2048,1024]{0,1:T(8,128)(2,1)} copy(bf16[2048,1024]{1,0:T(8,128)(2,1)} %convolution_convert_fusion) | data formatting | bytes 8388608 | tf_op jit(solution)/shard_map/convert_element_type | solution.py:60
  47.7 12.9 %reshape.33 = bf16[32,64,32,32]{1,0,3,2:T(8,128)(2,1)} reshape(bf16[2048,1024]{0,1:T(8,128)(2,1)} %copy.29) | data formatting | bytes 8388608 | tf_op jit(solution)/shard_map/reshape | solution.py:60
  62.3 5.7 %fusion.4 = f32[32,64,32]{1,2,0:T(8,128)S(1)} fusion(bf16[32,64,32,32]{1,0,3,2:T(8,128)(2,1)} %reshape.33, bf16[32,64,64,1]{2,1,0,3:T(8,128)(2,1)S(1)} %bitcast.71), kind=kOutput, calls=%fused_computation.8 | convolution fusion | flops 268500992 | bytes 4718592 | tf_op jit(solution)/shard_map/ijcd,dsj->csi/dot_general | solution.py:62
  68.0 0.9 copy.31
  68.9 1.2 reshape.47
  70.1 3.7 %all-to-all-start.1 = ((f32[16,1,4096]{2,1,0:T(1,128)}), f32[16,1,4096]{2,1,0:T(1,128)S(1)}, u32[]{:S(2)}, u32[]{:S(2)}) async-start(f32[16,1,4096]{2,1,0:T(1,128)} %reshape.47), calls=%async_computation.1 | async-start | bytes 524288 | tf_op jit(solution)/shard_map/all_to_all | solution.py:35
  73.8 5.5 %fusion = bf16[32,64,32,32]{1,0,2,3:T(8,128)(2,1)} fusion(bf16[32,64,64,1]{2,1,3,0:T(8,128)(2,1)S(1)} %bitcast.72, bf16[32,64,32]{1,2,0:T(8,128)(2,1)S(1)} %copy.35), kind=kOutput, calls=%fused_computation.1 | convolution fusion | flops 272629760 | bytes 4587520 | tf_op jit(solution)/shard_map/csi,dsj->ijcd/dot_general | solution.py:49
  79.4 9.1 %copy.36 = bf16[32,64,32,32]{1,0,3,2:T(8,128)(2,1)} copy(bf16[32,64,32,32]{1,0,2,3:T(8,128)(2,1)} %fusion) | data formatting | bytes 8388608 | tf_op jit(solution)/shard_map/convert_element_type | solution.py:50
  88.5 12.3 %reshape.38 = bf16[2048,1024]{0,1:T(8,128)(2,1)} reshape(bf16[32,64,32,32]{1,0,3,2:T(8,128)(2,1)} %copy.36) | data formatting | bytes 8388608 | tf_op jit(solution)/shard_map/reshape | solution.py:51
  100.8 4.2 %fusion.7 = f32[32,32,128]{2,1,0:T(8,128)} fusion(bf16[32,32,2048]{2,1,0:T(8,128)(2,1)} %bitcast.70, bf16[2048,128,1]{1,0,2:T(8,128)(2,1)S(1)} %bitcast.69), kind=kOutput, calls=%fused_computation.14 | convolution fusion | flops 536870912 | bytes 5242880 | tf_op jit(solution)/shard_map/dot_general | solution.py:54
  105.0 7.7 %all-to-all-start.4 = ((f32[32,32,128]{2,1,0:T(8,128)}), f32[32,32,128]{2,1,0:T(8,128)S(1)}, u32[]{:S(2)}, u32[]{:S(2)}) async-start(f32[32,32,128]{2,1,0:T(8,128)} %fusion.7), calls=%async_computation.4 | async-start | bytes 1048576 | tf_op jit(solution)/shard_map/all_to_all | solution.py:35
  112.8 8.3 %fusion.2 = f32[32,64,64]{1,2,0:T(8,128)} fusion(bf16[32,64,32,32]{1,0,3,2:T(8,128)(2,1)} %reshape.33, bf16[32,64,32,1]{2,0,1,3:T(8,128)(2,1)S(1)} %bitcast.76), kind=kOutput, calls=%fused_computation.5 | convolution fusion | flops 268566528 | bytes 4849664 | tf_op jit(solution)/shard_map/ijcd,csi->dsj/dot_general | solution.py:65
  121.0 2.1 %copy.34 = f32[32,64,64]{2,0,1:T(8,128)S(1)} copy(f32[32,64,64]{1,2,0:T(8,128)} %fusion.2) | data formatting | bytes 1048576 | tf_op jit(solution)/shard_map/div | solution.py:65
  123.2 1.4 reshape.51
  124.6 3.5 %all-to-all-done.4 = f32[32,32,128]{2,1,0:T(8,128)S(1)} async-done(((f32[32,32,128]{2,1,0:T(8,128)}), f32[32,32,128]{2,1,0:T(8,128)S(1)}, u32[]{:S(2)}, u32[]{:S(2)}) %all-to-all-start.4) | async-done | bytes 524320 | tf_op jit(solution)/shard_map/all_to_all | solution.py:35
  128.1 5.1 %all-to-all-start.3 = ((f32[32,1,4096]{2,1,0:T(1,128)}), f32[32,1,4096]{2,1,0:T(1,128)S(1)}, u32[]{:S(2)}, u32[]{:S(2)}) async-start(f32[32,1,4096]{2,1,0:T(1,128)} %reshape.51), calls=%async_computation.3 | async-start | bytes 1048576 | tf_op jit(solution)/shard_map/all_to_all | solution.py:35
  133.3 15.3 %all-to-all-done.3 = f32[32,1,4096]{2,1,0:T(1,128)S(1)} async-done(((f32[32,1,4096]{2,1,0:T(1,128)}), f32[32,1,4096]{2,1,0:T(1,128)S(1)}, u32[]{:S(2)}, u32[]{:S(2)}) %all-to-all-start.3) | async-done | bytes 524320 | tf_op jit(solution)/shard_map/all_to_all | solution.py:35
  148.7 0.7 broadcast_in_dim.8
  149.4 11.8 %all-to-all-start.5 = ((f32[16,32,128]{2,1,0:T(8,128)}), f32[16,32,128]{2,1,0:T(8,128)S(1)}, u32[]{:S(2)}, u32[]{:S(2)}) async-start(f32[16,32,128]{2,1,0:T(8,128)} %broadcast_in_dim.8), calls=%async_computation.5 | async-start | bytes 524288 | tf_op jit(solution)/shard_map/all_to_all | solution.py:11
  161.7 2.2 %reduce = f32[16,4096]{1,0:T(8,128)S(1)} reduce(f32[16,1,4096]{2,1,0:T(1,128)} %copy-done.1, f32[]{:T(128)} %broadcast.12), dimensions={1}, to_apply=%all_to_all.19.reduce_sub_computation | reduce | bytes 524292 | tf_op jit(solution)/shard_map/all_to_all | solution.py:35
  164.4 0.7 copy.37
  165.0 1.9 %reduce.1 = f32[32,4096]{1,0:T(8,128)S(1)} reduce(f32[32,1,4096]{2,1,0:T(1,128)S(1)} %all-to-all-done.3, f32[]{:T(128)} %broadcast.12), dimensions={1}, to_apply=%all_to_all.21.reduce_sub_computation | reduce | bytes 1048580 | tf_op jit(solution)/shard_map/all_to_all | solution.py:35
  167.5 0.6 copy.38
  168.1 9.5 %all-to-all-done.5 = f32[16,32,128]{2,1,0:T(8,128)S(1)} async-done(((f32[16,32,128]{2,1,0:T(8,128)}), f32[16,32,128]{2,1,0:T(8,128)S(1)}, u32[]{:S(2)}, u32[]{:S(2)}) %all-to-all-start.5) | async-done | bytes 262176 | tf_op jit(solution)/shard_map/all_to_all | solution.py:11
  (18 shorter events, 4.0 us)
Async XLA Ops:
  0.6 36.4 %copy-start = (bf16[32,64,128]{2,1,0:T(8,128)(2,1)S(1)}, bf16[32,64,128]{2,1,0:T(8,128)(2,1)}, u32[]{:S(2)}) copy-start(bf16[32,64,128]{2,1,0:T(8,128)(2,1)} %param.6) | copy-start | bytes 1572868
  2.7 28.2 %all-to-all-start.2 = ((bf16[16,2,2048]{2,1,0:T(2,128)(2,1)}), bf16[16,2,2048]{2,1,0:T(2,128)(2,1)S(1)}, u32[]{:S(2)}, u32[]{:S(2)}) async-start(bf16[16,2,2048]{2,1,0:T(2,128)(2,1)} %reshape.49), calls=%async_computation.2 | async-start | bytes 262144 | tf_op jit(solution)/shard_map/all_to_all | solution.py:11
  31.0 30.4 %all-to-all-start = ((bf16[32,2,2048]{2,1,0:T(2,128)(2,1)}), bf16[32,2,2048]{2,1,0:T(2,128)(2,1)S(1)}, u32[]{:S(2)}, u32[]{:S(2)}) async-start(bf16[32,2,2048]{2,1,0:T(2,128)(2,1)} %reshape.45), calls=%async_computation | async-start | bytes 524288 | tf_op jit(solution)/shard_map/all_to_all | solution.py:11
  70.1 34.9 %all-to-all-start.1 = ((f32[16,1,4096]{2,1,0:T(1,128)}), f32[16,1,4096]{2,1,0:T(1,128)S(1)}, u32[]{:S(2)}, u32[]{:S(2)}) async-start(f32[16,1,4096]{2,1,0:T(1,128)} %reshape.47), calls=%async_computation.1 | async-start | bytes 524288 | tf_op jit(solution)/shard_map/all_to_all | solution.py:35
  105.0 7.7 %copy-start.1 = (f32[16,1,4096]{2,1,0:T(1,128)}, f32[16,1,4096]{2,1,0:T(1,128)S(1)}, u32[]{:S(2)}) copy-start(f32[16,1,4096]{2,1,0:T(1,128)S(1)} %all-to-all-done.1) | copy-start | bytes 786436
  105.0 23.1 %all-to-all-start.4 = ((f32[32,32,128]{2,1,0:T(8,128)}), f32[32,32,128]{2,1,0:T(8,128)S(1)}, u32[]{:S(2)}, u32[]{:S(2)}) async-start(f32[32,32,128]{2,1,0:T(8,128)} %fusion.7), calls=%async_computation.4 | async-start | bytes 1048576 | tf_op jit(solution)/shard_map/all_to_all | solution.py:35
  128.1 20.5 %all-to-all-start.3 = ((f32[32,1,4096]{2,1,0:T(1,128)}), f32[32,1,4096]{2,1,0:T(1,128)S(1)}, u32[]{:S(2)}, u32[]{:S(2)}) async-start(f32[32,1,4096]{2,1,0:T(1,128)} %reshape.51), calls=%async_computation.3 | async-start | bytes 1048576 | tf_op jit(solution)/shard_map/all_to_all | solution.py:35
  149.4 28.2 %all-to-all-start.5 = ((f32[16,32,128]{2,1,0:T(8,128)}), f32[16,32,128]{2,1,0:T(8,128)S(1)}, u32[]{:S(2)}, u32[]{:S(2)}) async-start(f32[16,32,128]{2,1,0:T(8,128)} %broadcast_in_dim.8), calls=%async_computation.5 | async-start | bytes 524288 | tf_op jit(solution)/shard_map/all_to_all | solution.py:11
where the time goes:
time: 180 us; the launch traced here: 178 us
  local copies, waits for them, and re-layouts  55.9 us (31%)
  starting transfers between devices  49.2 us (27%)
  waiting for transfers between devices  39.5 us (22%)
  matrix products  27.8 us (15%)
  other arithmetic  4.98 us (3%)
    all_to_all x3, starting transfers between devices, sent_to_all(): lax.all_to_all(jnp.broadcast_to(shard[None], (count, *shard.shape)), axis...  32.6 us
    all_to_all x3, waiting for transfers between devices, sent_to_all(): lax.all_to_all(jnp.broadcast_to(shard[None], (count, *shard.shape)), axis...  20.7 us
    all_to_all x3, waiting for transfers between devices, summed_on_arrival(): tiles = lax.all_to_all(in_blocks(shard, dim, count), axis, 0, 0, tiled=True)  18.8 us
    all_to_all x3, starting transfers between devices, summed_on_arrival(): tiles = lax.all_to_all(in_blocks(shard, dim, count), axis, 0, 0, tiled=True)  16.6 us
    reshape x1, local copies, waits for them, and re-layouts, body(): grad_outer.astype(jnp.bfloat16).reshape(first, second, chans, chans)  12.9 us
    reshape x1, local copies, waits for them, and re-layouts, body(): outer_flat = outer.reshape(first * second, chans * chans)  12.3 us
    convert_element_type x1, local copies, waits for them, and re-layouts, body(): outer = (jnp.einsum('csi,dsj->ijcd', left, right, preferred_element_type=...  9.11 us
    unnamed x16, local copies, waits for them, and re-layouts  8.49 us
  transfers between devices with their start and end apart: 6, of which 4 were waited for; matrix products, arithmetic and copies ran while one was open for 43% of the time, Pallas kernels for 0%

commit v1 on v0

v1 whole, which is shorter than its diff:
```python
import jax
import jax.numpy as jnp
from jax import lax
from jax.experimental import pallas as pl
from jax.experimental.pallas import tpu as pltpu
from jax.sharding import PartitionSpec as P

BF = jnp.bfloat16
F32 = jnp.float32
MESH = pl.DeviceIdType.MESH
S = 64
C = 32
Q = 16
Z = 8


def dot(a, b, dims=((1,), (0,))):
    return lax.dot_general(a, b, (dims, ((), ())), preferred_element_type=F32)


def kernel(
    rmsg, lmsg, g, w,
    gl_out, gr_out, gw_out,
    rbuf, lbuf, fr, fl, wf, wp, lt, l2, bd, xb, yb,
    gws, gwp, gwh, gwsend, gwrecv, gwz, gwzs, gwy, gwys,
    grs, grp, grh, grsend, grrecv,
    gls, glsend, glrecv, gly, glys,
    rs, rr, ls, lf, lr, pair_s, pair_r, ws, wr, gs, gr, zws, zwr, zls, zlr, ys, yr,
):
    row, col = lax.axis_index("row"), lax.axis_index("col")
    core, q = lax.rem(row, 2), row // 2
    yh, z = lax.rem(col, 2), col // 2
    pair = (row + 1 - 2 * core, col)
    other = (row, col + 1 - 2 * yh)

    def chip(k):
        return lax.rem(q + k, Q)

    def level(k):
        return lax.rem(z + k, Z)

    def row_mate(k):
        return (2 * chip(k) + core, col)

    def z_mate(k):
        return (row, 2 * level(k) + yh)

    def remote(src, dst, send, recv, device):
        return pltpu.make_async_remote_copy(
            src_ref=src, dst_ref=dst, send_sem=send, recv_sem=recv,
            device_id=device, device_id_type=MESH,
        )

    def each(first, last, step):
        def body(k, carry):
            step(k)
            return carry

        lax.fori_loop(first, last, body, 0)

    barrier = pltpu.get_barrier_semaphore()

    def greet(device):
        pl.semaphore_signal(barrier, inc=1, device_id=device, device_id_type=MESH)

    greet(pair)
    greet(other)
    each(1, Q, lambda k: greet(row_mate(k)))
    each(1, Z, lambda k: greet(z_mate(k)))

    wf[...] = w[...].astype(F32)

    def order_weight(d):
        for half in range(2):
            rows = wf[pl.ds(half * C + d, Q, stride=2 * C), :]
            wp[pl.ds(pl.multiple_of(d * C + half * Q, Q), Q), :] = rows.astype(BF)

    each(0, C, order_weight)
    rbuf[core, q] = rmsg[...]
    lbuf[col] = lmsg[...]

    pl.semaphore_wait(barrier, Q + Z)

    def r_copy(k, slot):
        return remote(rmsg, rbuf.at[core, slot], rs.at[k], rr.at[slot], row_mate(k))

    def l_copy(k, slot):
        return remote(lmsg, lbuf.at[slot], ls.at[k], lr.at[slot], z_mate(k))

    def l_side(slot):
        return remote(lmsg, lbuf.at[slot], ls.at[0], lr.at[slot], other)

    l_side(col).start()
    each(1, Q, lambda k: r_copy(k, q).start())
    each(1, Z, lambda k: l_copy(k, col).start())

    def grad_outer(p):
        gp = g[pl.ds(pl.multiple_of(p * 256, 256), 256), :]
        y = dot(wp[...], gp, ((1,), (1,))).astype(BF)
        yb[2 * p] = y[:, :128].reshape(C, C, 128)
        yb[2 * p + 1] = y[:, 128:].reshape(C, C, 128)

    each(0, 8, grad_outer)

    side_col = col + 1 - 2 * yh
    l_side(side_col).wait_recv()

    def l_forward(k, slot):
        return remote(lbuf.at[slot], lbuf.at[slot], lf.at[k], lr.at[slot], z_mate(k))

    each(1, Z, lambda k: l_forward(k, side_col).start())

    each(1, Q, lambda k: r_copy(k, chip(k)).wait_recv())

    def r_pair(half):
        return remote(rbuf.at[half], rbuf.at[half], pair_s.at[0], pair_r.at[0], pair)

    r_pair(core).start()

    def l_wait(k):
        l_copy(k, 2 * level(k) + yh).wait_recv()
        l_forward(k, 2 * level(k) + 1 - yh).wait_recv()

    each(1, Z, l_wait)
    fl[...] = lbuf[...].reshape(Q * 32, 128).astype(F32)
    for tile in range(4):
        parts = [fl[pl.ds(tile * 8 + r, Q, stride=32), :] for r in range(8)]
        block = jnp.concatenate(parts, axis=0)
        lt[:, tile * 128 : (tile + 1) * 128] = block.astype(BF)
        l2[tile * 128 : (tile + 1) * 128, :] = (block.T * (1.0 / S)).astype(BF)

    r_pair(1 - core).wait_recv()
    fr[...] = rbuf[...].reshape(2 * Q * 32, 128).astype(F32)
    low = lax.broadcasted_iota(jnp.int32, (S, 128), 1) < 64

    def make_blocks(t):
        parts = [
            fr[pl.ds(half * 512 + 2 * t + s, Q, stride=32), :] for half in range(2) for s in range(2)
        ]
        v = jnp.concatenate(parts, axis=0)
        u = pltpu.roll(v, 64, 1)
        zero = jnp.zeros_like(v)
        bd[t, :S, :128] = jnp.where(low, v, zero).astype(BF)
        bd[t, :S, 128:] = jnp.where(low, u, zero).astype(BF)
        bd[t, S:, :128] = jnp.where(low, zero, u).astype(BF)
        bd[t, S:, 128:] = jnp.where(low, zero, v).astype(BF)

    def outer(t):
        x = dot(l2[...], bd[t]).astype(BF)
        xb[:, 2 * t] = x[:, :128].reshape(Q, C, 128)
        xb[:, 2 * t + 1] = x[:, 128:].reshape(Q, C, 128)

    def some(count, step):
        def body(n):
            for m in range(count):
                step(n * count + m)

        return body

    each(0, 4, some(4, make_blocks))
    each(0, 4, some(4, outer))

    def grad_w(n):
        total = None
        for p in range(8):
            a = xb[2 * p, pl.ds(n * 8, 8)].reshape(256, 128)
            b = xb[2 * p + 1, pl.ds(n * 8, 8)].reshape(256, 128)
            term = dot(jnp.concatenate([a, b], axis=1), g[p * 256 : (p + 1) * 256, :])
            total = term if total is None else total + term
        gws[pl.ds(n * 8, 8)] = total.reshape(8, C, 128)

    each(0, 4, grad_w)

    def w_pair(half):
        src = gws.at[:, pl.ds(pl.multiple_of(half * Q, Q), Q), :]
        return remote(src, gwp, pair_s.at[1], pair_r.at[1], pair)

    w_pair(1 - core).start()

    def grad_r(t):
        y = jnp.concatenate([yb[:, 2 * t].reshape(512, 128), yb[:, 2 * t + 1].reshape(512, 128)], axis=1)
        x = dot(lt[...], y)
        a, b = x[:S, :128], x[S:, :128]
        c, d = x[:S, 128:], x[S:, 128:]
        grs[t] = jnp.where(low, a, d) + pltpu.roll(jnp.where(low, c, b), 64, 1)

    each(0, 4, some(4, grad_r))

    def g_pair(half):
        src = grs.at[:, pl.ds(pl.multiple_of(half * 32, 32), 32), :]
        return remote(src, grp, pair_s.at[2], pair_r.at[2], pair)

    g_pair(1 - core).start()

    def row_sends(sums, send_buf, recv_buf, send_sem, recv_sem):
        def fill(k):
            slot = chip(k)
            send_buf[slot] = sums[pl.ds(slot, 32, stride=Q), :].astype(BF)

        each(1, Q, fill)
        each(
            1, Q,
            lambda k: remote(
                send_buf.at[chip(k)], recv_buf.at[q], send_sem.at[k], recv_sem.at[q], row_mate(k)
            ).start(),
        )

    def row_wait(send_buf, recv_buf, send_sem, recv_sem):
        def one(k):
            remote(
                send_buf.at[chip(k)], recv_buf.at[chip(k)], send_sem.at[k], recv_sem.at[chip(k)], row_mate(k)
            ).wait_recv()

        each(1, Q, one)

    def row_total(sums, recv_buf):
        def add(k, acc):
            return acc + recv_buf[chip(k)].astype(F32)

        return lax.fori_loop(1, Q, add, sums[pl.ds(q, 32, stride=Q), :])

    w_pair(core).wait_recv()
    gwh[...] = (gws[:, pl.ds(pl.multiple_of(core * Q, Q), Q), :] + gwp[...]).reshape(512, 128)
    row_sends(gwh, gwsend, gwrecv, ws, wr)

    for tile in range(4):
        gls[tile] = jnp.zeros((128, 128), F32)

    def grad_l(n):
        total = None
        for m in range(4):
            t = n * 4 + m
            y = jnp.concatenate(
                [yb[:, 2 * t].reshape(512, 128), yb[:, 2 * t + 1].reshape(512, 128)], axis=1
            )
            term = dot(bd[t], y, ((1,), (1,)))
            total = term if total is None else total + term
        for tile in range(4):
            gls[tile] += total[:, tile * 128 : (tile + 1) * 128]

    each(0, 4, grad_l)

    g_pair(core).wait_recv()
    grh[...] = (grs[:, pl.ds(pl.multiple_of(core * 32, 32), 32), :] + grp[...]).reshape(512, 128)
    row_sends(grh, grsend, grrecv, gs, gr)

    def l_rows(c):
        return jnp.concatenate([gls[tile, pl.ds(c, 8, stride=Q), :] for tile in range(4)], axis=0)

    def fill_l(k):
        for side in range(2):
            glsend[level(k), side] = l_rows(2 * level(k) + side).astype(BF)

    each(1, Z, fill_l)

    def l_reduce(k, slot):
        return remote(glsend.at[level(k)], glrecv.at[slot], zls.at[k], zlr.at[slot], z_mate(k))

    each(1, Z, lambda k: l_reduce(k, z).start())

    row_wait(gwsend, gwrecv, ws, wr)
    total_w = row_total(gwh, gwrecv).astype(BF)
    gwzs[...] = total_w
    gwz[z] = total_w

    def w_level(k, slot):
        return remote(gwzs, gwz.at[slot], zws.at[k], zwr.at[slot], z_mate(k))

    each(1, Z, lambda k: w_level(k, z).start())

    each(1, Z, lambda k: l_reduce(k, level(k)).wait_recv())

    def l_total(side):
        def add(k, acc):
            return acc + glrecv[level(k), side].astype(F32)

        return lax.fori_loop(1, Z, add, l_rows(2 * z + side))

    glys[...] = l_total(1 - yh)
    side_l = remote(glys, gly, ys.at[0], yr.at[0], other)
    side_l.start()
    mine_l = l_total(yh)

    row_wait(grsend, grrecv, gs, gr)
    gr_out[...] = row_total(grh, grrecv) * (1.0 / S)

    each(1, Z, lambda k: w_level(k, level(k)).wait_recv())
    acc = gwz[0].astype(F32)
    for n in range(1, Z):
        acc = acc + gwz[n].astype(F32)
    gwys[...] = acc
    side_w = remote(gwys, gwy, ys.at[1], yr.at[1], other)
    side_w.start()

    side_l.wait_recv()
    gl_out[...] = (mine_l + gly[...]) * (1.0 / S)
    side_w.wait_recv()
    gw_out[...] = acc + gwy[...]

    l_side(col).wait_send()

    def finish_row(k):
        r_copy(k, q).wait_send()
        remote(gwsend.at[chip(k)], gwrecv.at[q], ws.at[k], wr.at[q], row_mate(k)).wait_send()
        remote(grsend.at[chip(k)], grrecv.at[q], gs.at[k], gr.at[q], row_mate(k)).wait_send()

    def finish_z(k):
        l_copy(k, col).wait_send()
        l_forward(k, side_col).wait_send()
        l_reduce(k, z).wait_send()
        w_level(k, z).wait_send()

    each(1, Q, finish_row)
    each(1, Z, finish_z)
    r_pair(core).wait_send()
    w_pair(1 - core).wait_send()
    g_pair(1 - core).wait_send()
    side_l.wait_send()
    side_w.wait_send()


def body(left_act, right_act, cotangent, weight):
    rmsg = right_act.reshape(16, 2, 2, 64).transpose(0, 2, 1, 3).reshape(32, 128)
    lmsg = left_act.reshape(16, 2, 4, 4, 4, 2).transpose(3, 5, 2, 4, 1, 0).reshape(32, 128)
    vm = pltpu.VMEM
    dma = pltpu.SemaphoreType.DMA
    msg = (32, 128)
    gl, gr, gw = pl.pallas_call(
        kernel,
        out_shape=[jax.ShapeDtypeStruct(msg, F32)] * 3,
        in_specs=[pl.BlockSpec(memory_space=vm)] * 4,
        out_specs=[pl.BlockSpec(memory_space=vm)] * 3,
        scratch_shapes=[
            vm((2, Q, *msg), BF), vm((16, *msg), BF),
            vm((1024, 128), F32), vm((512, 128), F32), vm((1024, 128), F32), vm((1024, 128), BF),
            vm((128, 512), BF), vm((512, 128), BF), vm((16, 128, 256), BF),
            vm((16, C, C, 128), BF), vm((16, C, C, 128), BF),
            vm((C, C, 128), F32), vm((C, Q, 128), F32), vm((512, 128), F32),
            vm((Q, *msg), BF), vm((Q, *msg), BF), vm((Z, *msg), BF), vm(msg, BF), vm(msg, F32), vm(msg, F32),
            vm((16, S, 128), F32), vm((16, 32, 128), F32), vm((512, 128), F32),
            vm((Q, *msg), BF), vm((Q, *msg), BF),
            vm((4, 128, 128), F32), vm((Z, 2, *msg), BF), vm((Z, 2, *msg), BF), vm(msg, F32), vm(msg, F32),
            dma((Q,)), dma((Q,)), dma((Z,)), dma((Z,)), dma((16,)), dma((3,)), dma((3,)),
            dma((Q,)), dma((Q,)), dma((Q,)), dma((Q,)),
            dma((Z,)), dma((Z,)), dma((Z,)), dma((Z,)), dma((2,)), dma((2,)),
        ],
        compiler_params=pltpu.CompilerParams(collective_id=0, has_side_effects=True),
    )(rmsg, lmsg, cotangent.reshape(2048, 128), weight)
    grad_left = gl.reshape(4, 2, 4, 4, 2, 16).transpose(5, 4, 2, 0, 3, 1).reshape(32, 4, 32)
    grad_right = gr.reshape(16, 2, 2, 64).transpose(0, 2, 1, 3).reshape(32, 2, 64)
    return grad_left, grad_right, gw


def solution(mesh):
    return jax.shard_map(
        body,
        mesh=mesh,
        in_specs=(P(None, "col", "row"), P(None, "row", "col"), P("row", "col", None), P()),
        out_specs=(P(None, "col", "row"), P(None, "row", "col"), P("row", None)),
        check_vma=False,
    )
```

time: 180 us -> 55.8 us (0.31)
  the two profiles are of different devices: /device:TPU:8 before, /device:TPU:14 now
where the time goes in v1:
time: 55.8 us; the launch traced here: 55.4 us
  Pallas kernels  47.7 us (85%)
  local copies, waits for them, and re-layouts  7.03 us (13%)
  between operations  0.68 us (1%)
    pallas_call x1, Pallas kernels, body(): pl.pallas_call(kernel, out_shape=[jax.ShapeDtypeStruct(msg, F32)] * 3, in...  47.7 us
    unnamed x9, local copies, waits for them, and re-layouts  2.65 us
    reshape x2, local copies, waits for them, and re-layouts, body(): gl.reshape(4, 2, 4, 4, 2, 16).transpose(5, 4, 2, 0, 3, 1).reshape(32, 4, 32)  1.75 us

profile of v1, /device:TPU:14, one launch (start us, length us, event | category | flops | bytes accessed | tf_op | source)
XLA Modules:
  0.0 55.4 jit_solution(5380407180444140797)
XLA Ops:
  0.6 1.1 %copy.12 = bf16[32,4,32]{1,2,0:T(8,128)(2,1)S(1)} copy(bf16[32,4,32]{2,1,0:T(4,128)(2,1)} %param.4) | data formatting | bytes 16384 | tf_op args[0]
  1.7 0.5 copy.13
  2.2 0.0 copy-start.1
  2.2 0.7 %reshape.36.lmsg = bf16[32,128]{1,0:T(8,128)(2,1)} reshape(bf16[4,2,4,4,2,16]{5,4,3,2,1,0:T(2,128)(2,1)S(1)} %copy.13) | data formatting | bytes 16384 | tf_op jit(solution)/shard_map/reshape | solution.py:324
  2.9 0.0 copy-done.1
  2.9 0.7 %reshape.34.rmsg = bf16[32,128]{1,0:T(8,128)(2,1)} reshape(bf16[16,2,2,64]{3,2,1,0:T(2,128)(2,1)S(1)} %bitcast.17) | data formatting | bytes 16384 | tf_op jit(solution)/shard_map/reshape | solution.py:323
  3.6 47.7 %shard_map.67 = (f32[32,128]{1,0:T(8,128)}, f32[32,128]{1,0:T(8,128)}, f32[32,128]{1,0:T(8,128)}) custom-call(bf16[32,128]{1,0:T(8,128)(2,1)} %reshape.34.rmsg, bf16[32,128]{1,0:T(8,128)(2,1)} %reshape.36.lmsg, bf16[2048,128]{1,0:T(8,128)(2,1)} %bitcast.15, bf16[1024,128]{1,0:T(8,128)(2,1)} %w.1), custom_call_target="tpu_custom_call" | custom-call | tf_op jit(solution)/shard_map/pallas_call | solution.py:328
  51.3 0.9 %reshape.38 = f32[4,2,4,4,2,16]{5,4,3,2,1,0:T(2,128)S(1)} reshape(f32[32,128]{1,0:T(8,128)} %get-tuple-element.6) | data formatting | bytes 32768 | tf_op jit(solution)/shard_map/reshape | solution.py:349
  52.2 0.8 %copy.14 = f32[4,2,4,4,2,16]{2,1,3,0,4,5:T(2,128)S(1)} copy(f32[4,2,4,4,2,16]{5,4,3,2,1,0:T(2,128)S(1)} %reshape.38) | data formatting | bytes 32768 | tf_op jit(solution)/shard_map/reshape | solution.py:349
  53.1 0.0 copy-start
  53.1 0.9 %copy.16 = f32[32,4,32]{2,1,0:T(4,128)} copy(f32[32,4,32]{1,2,0:T(8,128)S(1)} %bitcast.13) | data formatting | bytes 32768
  54.0 0.0 copy-done
  54.0 0.1 reshape.40
  54.1 0.0 copy-start.2
  54.1 0.6 %copy.15 = f32[16,2,2,64]{3,2,1,0:T(2,128)} copy(f32[16,2,2,64]{3,1,2,0:T(2,128)S(1)} %bitcast.16) | data formatting | bytes 32768 | tf_op jit(solution)/shard_map/transpose | solution.py:350
  54.7 0.1 copy-done.2
  54.8 0.6 %copy.20 = f32[32,128]{1,0:T(8,128)} copy(f32[32,128]{1,0:T(8,128)S(1)} %copy-done.2) | data formatting | bytes 32768
  (1 shorter events, 0.0 us)
Async XLA Ops:
  2.2 0.7 %copy-start.1 = (bf16[32,2,64]{2,1,0:T(2,128)(2,1)S(1)}, bf16[32,2,64]{2,1,0:T(2,128)(2,1)}, u32[]{:S(2)}) copy-start(bf16[32,2,64]{2,1,0:T(2,128)(2,1)} %param.5) | copy-start | bytes 24580
  53.1 0.9 %copy-start = (f32[32,128]{1,0:T(8,128)S(1)}, f32[32,128]{1,0:T(8,128)}, u32[]{:S(2)}) copy-start(f32[32,128]{1,0:T(8,128)} %get-tuple-element.7) | copy-start | bytes 49156
  54.1 0.7 %copy-start.2 = (f32[32,128]{1,0:T(8,128)S(1)}, f32[32,128]{1,0:T(8,128)}, u32[]{:S(2)}) copy-start(f32[32,128]{1,0:T(8,128)} %get-tuple-element.17) | copy-start | bytes 49156

commit v2 on v1

v2 whole, which is shorter than its diff:
```python
import jax
import jax.numpy as jnp
from jax import lax
from jax.experimental import pallas as pl
from jax.experimental.pallas import tpu as pltpu
from jax.sharding import PartitionSpec as P

BF = jnp.bfloat16
F32 = jnp.float32
MESH = pl.DeviceIdType.MESH
S = 64
C = 32
Q = 16
Z = 8
R_ROW, R_PAIR, L_SIDE, L_LEVEL, W_PAIR, W_ROW, W_LEVEL, G_PAIR, G_ROW, L_SUM, L_SUM_SIDE, W_SIDE = range(12)


def dot(a, b, dims=((1,), (0,))):
    return lax.dot_general(a, b, (dims, ((), ())), preferred_element_type=F32)


def swap_groups(parts, group):
    outs = []
    for s in range(4):
        out = None
        for a in range(4):
            shift = (a - s) % 4 * 32
            moved = pltpu.roll(parts[a], shift, 1) if shift else parts[a]
            out = moved if out is None else jnp.where(group == a, moved, out)
        outs.append(out)
    return outs


def kernel(
    l_in, r_in, g_in, w_in,
    gl_out, gr_out, gw_out,
    lv, rv, g, w, ra, la, lb, rmsg, lmsg,
    rbuf, lbuf, fr, fl, wf, wp, lt, l2, bd, xb, yb,
    gws, gwp, gwh, gwsend, gwrecv, gwz, gwzs, gwy, gwys,
    grs, grp, grh, grsend, grrecv, grf,
    gls, glsend, glrecv, gly, glys, glf, gt, ga,
    gwo, gro, glo, in_sem, out_sem, sent, got,
):
    row, col = lax.axis_index("row"), lax.axis_index("col")
    core, q = lax.rem(row, 2), row // 2
    yh, z = lax.rem(col, 2), col // 2
    pair = (row + 1 - 2 * core, col)
    other = (row, col + 1 - 2 * yh)

    def chip(k):
        return lax.rem(q + k, Q)

    def level(k):
        return lax.rem(z + k, Z)

    def row_mate(k):
        return (2 * chip(k) + core, col)

    def z_mate(k):
        return (row, 2 * level(k) + yh)

    def remote(src, dst, n, device):
        return pltpu.make_async_remote_copy(
            src_ref=src, dst_ref=dst, send_sem=sent.at[n], recv_sem=got.at[n],
            device_id=device, device_id_type=MESH,
        )

    def batch(buf, count, n):
        part = buf.at[pl.ds(0, count)]
        return remote(part, part, n, pair)

    def each(first, last, step):
        def body(k, carry):
            step(k)
            return carry

        lax.fori_loop(first, last, body, 0)

    barrier = pltpu.get_barrier_semaphore()

    def greet(device):
        pl.semaphore_signal(barrier, inc=1, device_id=device, device_id_type=MESH)

    each(1, Q, lambda k: greet(row_mate(k)))
    greet(other)
    each(1, Z, lambda k: greet(z_mate(k)))
    greet(pair)

    copies = [
        pltpu.make_async_copy(src, dst, in_sem.at[n])
        for n, (src, dst) in enumerate([(r_in, rv), (l_in, lv), (w_in, w), (g_in, g)])
    ]
    for copy in copies:
        copy.start()

    lane = lax.broadcasted_iota(jnp.int32, (S, 128), 1)
    low = lane < 64
    group = lane[:8] // 32

    ra[...] = jnp.zeros_like(ra)
    la[...] = jnp.zeros_like(la)
    copies[0].wait()
    for d in range(C):
        ra[2 * d : 2 * d + 2, :64] = rv[d].astype(F32)
    for s in range(2):
        a = ra[pl.ds(s, 16, stride=4), :]
        b = ra[pl.ds(2 + s, 16, stride=4), :]
        rmsg[s * 16 : s * 16 + 16, :] = jnp.where(low[:16], a, pltpu.roll(b, 64, 1)).astype(BF)

    copies[1].wait()
    for c in range(C):
        la[4 * c : 4 * c + 4, :32] = lv[c].astype(F32)
    stack = [la[pl.ds(half * 4 + s, Q, stride=8), :] for s in range(4) for half in range(2)]
    lb[...] = jnp.concatenate(stack, axis=0).T[:32]
    parts = [
        jnp.concatenate([lb[pl.ds(2 * a + n, 4, stride=8), :] for n in range(2)], axis=0)
        for a in range(4)
    ]
    lmsg[...] = jnp.concatenate(swap_groups(parts, group), axis=0).astype(BF)
    rbuf[core, q] = rmsg[...]
    lbuf[col] = lmsg[...]

    pl.semaphore_wait(barrier, Q + Z)

    side_col = col + 1 - 2 * yh
    l_side = remote(lmsg, lbuf.at[col], L_SIDE, other)
    l_side.start()
    each(1, Z, lambda k: remote(lmsg, lbuf.at[col], L_LEVEL, z_mate(k)).start())
    r_slots = rbuf.at[core]
    each(1, Q, lambda k: remote(rmsg, r_slots.at[q], R_ROW, row_mate(k)).start())

    copies[2].wait()
    wf[...] = w[...].astype(F32)

    def order_weight(d):
        for half in range(2):
            rows = wf[pl.ds(half * C + d, Q, stride=2 * C), :]
            wp[pl.ds(pl.multiple_of(d * C + half * Q, Q), Q), :] = rows.astype(BF)

    def some(count, step):
        def body(n):
            for m in range(count):
                step(n * count + m)

        return body

    each(0, C // 8, some(8, order_weight))
    copies[3].wait()

    def grad_outer(p):
        gp = g[pl.ds(pl.multiple_of(p * 256, 256), 256), :]
        y = dot(wp[...], gp, ((1,), (1,))).astype(BF)
        yb[2 * p] = y[:, :128].reshape(C, C, 128)
        yb[2 * p + 1] = y[:, 128:].reshape(C, C, 128)

    each(0, 8, grad_outer)

    l_side.wait_recv()
    forward = lbuf.at[side_col]
    each(1, Z, lambda k: remote(forward, forward, L_LEVEL, z_mate(k)).start())

    batch(r_slots, Q - 1, R_ROW).wait_recv()
    r_pair = remote(r_slots, r_slots, R_PAIR, pair)
    r_pair.start()

    r_pair.wait_recv()
    fr[...] = rbuf[...].reshape(2 * Q * 32, 128).astype(F32)

    def make_blocks(t):
        rows = [
            fr[pl.ds(half * 512 + s * 16 + t, Q, stride=32), :] for half in range(2) for s in range(2)
        ]
        v = jnp.concatenate(rows, axis=0)
        u = pltpu.roll(v, 64, 1)
        zero = jnp.zeros_like(v)
        bd[t, :S, :128] = jnp.where(low, v, zero).astype(BF)
        bd[t, :S, 128:] = jnp.where(low, u, zero).astype(BF)
        bd[t, S:, :128] = jnp.where(low, zero, u).astype(BF)
        bd[t, S:, 128:] = jnp.where(low, zero, v).astype(BF)

    each(0, 4, some(4, make_blocks))

    batch(lbuf, 2 * (Z - 1), L_LEVEL).wait_recv()
    fl[...] = lbuf[...].reshape(Q * 32, 128).astype(F32)
    for tile in range(4):
        rows = [
            fl[pl.ds(s * 8 + n * 4 + tile, Q, stride=32), :] for n in range(2) for s in range(4)
        ]
        block = jnp.concatenate(rows, axis=0)
        lt[:, tile * 128 : (tile + 1) * 128] = block.astype(BF)
        l2[tile * 128 : (tile + 1) * 128, :] = (block.T * (1.0 / S)).astype(BF)

    def outer(t):
        x = dot(l2[...], bd[t]).astype(BF)
        xb[:, 2 * t] = x[:, :128].reshape(Q, C, 128)
        xb[:, 2 * t + 1] = x[:, 128:].reshape(Q, C, 128)

    def grad_w(n):
        total = None
        for p in range(8):
            a = xb[2 * p, pl.ds(n * 8, 8)].reshape(256, 128)
            b = xb[2 * p + 1, pl.ds(n * 8, 8)].reshape(256, 128)
            term = dot(jnp.concatenate([a, b], axis=1), g[p * 256 : (p + 1) * 256, :])
            total = term if total is None else total + term
        gws[pl.ds(n * 8, 8)] = total.reshape(8, C, 128)

    for t in range(16):
        outer(t)
    for n in range(4):
        grad_w(n)
    w_pair = remote(gws.at[:, pl.ds(pl.multiple_of((1 - core) * Q, Q), Q), :], gwp, W_PAIR, pair)
    w_pair.start()

    def grad_r(t):
        y = jnp.concatenate([yb[:, 2 * t].reshape(512, 128), yb[:, 2 * t + 1].reshape(512, 128)], axis=1)
        x = dot(lt[...], y)
        a, b = x[:S, :128], x[S:, :128]
        c, d = x[:S, 128:], x[S:, 128:]
        grs[t] = jnp.where(low, a, d) + pltpu.roll(jnp.where(low, c, b), 64, 1)

    each(0, 2, some(4, grad_r))
    w_pair.wait_recv()
    gwh[...] = (gws[:, pl.ds(pl.multiple_of(core * Q, Q), Q), :] + gwp[...]).reshape(512, 128)

    def fill_w(k):
        gwsend[k] = gwh[pl.ds(k, 32, stride=Q), :].astype(BF)

    each(0, 2, some(8, fill_w))
    each(1, Q, lambda k: remote(gwsend.at[chip(k)], gwrecv.at[q], W_ROW, row_mate(k)).start())
    each(2, 4, some(4, grad_r))

    g_pair = remote(grs.at[:, pl.ds(pl.multiple_of((1 - core) * 32, 32), 32), :], grp, G_PAIR, pair)
    g_pair.start()

    for tile in range(4):
        gls[tile] = jnp.zeros((128, 128), F32)

    def grad_l(n):
        total = None
        for m in range(4):
            t = n * 4 + m
            y = jnp.concatenate(
                [yb[:, 2 * t].reshape(512, 128), yb[:, 2 * t + 1].reshape(512, 128)], axis=1
            )
            term = dot(bd[t], y, ((1,), (1,)))
            total = term if total is None else total + term
        for tile in range(4):
            gls[tile] += total[:, tile * 128 : (tile + 1) * 128]

    each(0, 4, grad_l)

    g_pair.wait_recv()
    grh[...] = (grs[:, pl.ds(pl.multiple_of(core * 32, 32), 32), :] + grp[...]).reshape(512, 128)

    def fill_g(k):
        grsend[chip(k)] = grh[pl.ds(chip(k), 32, stride=Q), :].astype(BF)

    each(0, 4, some(4, fill_g))
    each(1, Q, lambda k: remote(grsend.at[chip(k)], grrecv.at[q], G_ROW, row_mate(k)).start())

    def l_rows(c):
        return jnp.concatenate([gls[tile, pl.ds(c, 8, stride=Q), :] for tile in range(4)], axis=0)

    def fill_l(k):
        for side in range(2):
            glsend[level(k), side] = l_rows(2 * level(k) + side).astype(BF)

    each(0, 2, some(4, fill_l))

    each(1, Z, lambda k: remote(glsend.at[level(k)], glrecv.at[z], L_SUM, z_mate(k)).start())

    batch(gwrecv, Q - 1, W_ROW).wait_recv()
    acc = gwh[pl.ds(q, 32, stride=Q), :]
    for k in range(1, Q):
        acc = acc + gwrecv[chip(k)].astype(F32)
    total_w = acc.astype(BF)
    gwzs[...] = total_w
    gwz[z] = total_w
    each(1, Z, lambda k: remote(gwzs, gwz.at[z], W_LEVEL, z_mate(k)).start())

    batch(glrecv, Z - 1, L_SUM).wait_recv()

    def l_total(side):
        acc = l_rows(2 * z + side)
        for k in range(1, Z):
            acc = acc + glrecv[level(k), side].astype(F32)
        return acc

    glys[...] = l_total(1 - yh)
    side_l = remote(glys, gly, L_SUM_SIDE, other)
    side_l.start()
    glf[...] = l_total(yh)

    batch(grrecv, Q - 1, G_ROW).wait_recv()
    acc_r = grh[pl.ds(q, 32, stride=Q), :]
    for k in range(1, Q):
        acc_r = acc_r + grrecv[chip(k)].astype(F32)
    acc_r = acc_r * (1.0 / S)
    grf[0] = acc_r
    grf[1] = pltpu.roll(acc_r, 64, 1)
    for t in range(16):
        for dd in range(2):
            gro[2 * t + dd] = grf[dd, 2 * t : 2 * t + 2, :64]
    put_r = pltpu.make_async_copy(gro, gr_out, out_sem.at[0])
    put_r.start()

    gt[...] = jnp.zeros_like(gt)
    batch(gwz, Z - 1, W_LEVEL).wait_recv()
    acc = gwz[0].astype(F32)
    for n in range(1, Z):
        acc = acc + gwz[n].astype(F32)
    gwys[...] = acc
    side_w = remote(gwys, gwy, W_SIDE, other)
    side_w.start()
    side_l.wait_recv()
    glf[...] = (glf[...] + gly[...]) * (1.0 / S)
    parts = swap_groups([glf[pl.ds(s, 8, stride=4), :] for s in range(4)], group)
    for a in range(4):
        for tile in range(4):
            gt[tile * 8 + 2 * a : tile * 8 + 2 * a + 2, :] = parts[a][2 * tile : 2 * tile + 2]
    ga[...] = gt[...].T
    for c in range(C):
        glo[c] = ga[pl.ds(c % 2 * Q + c // 2, 4, stride=32), :][:, :32]
    put_l = pltpu.make_async_copy(glo, gl_out, out_sem.at[1])
    put_l.start()

    side_w.wait_recv()
    gwo[...] = gwys[...] + gwy[...]
    put_w = pltpu.make_async_copy(gwo, gw_out, out_sem.at[2])
    put_w.start()

    batch(r_slots, Q - 1, R_ROW).wait_send()
    l_side.wait_send()
    batch(lbuf, 2 * (Z - 1), L_LEVEL).wait_send()
    r_pair.wait_send()
    w_pair.wait_send()
    batch(gwrecv, Q - 1, W_ROW).wait_send()
    side_w.wait_send()
    g_pair.wait_send()
    batch(grsend, Q - 1, G_ROW).wait_send()
    batch(glsend, Z - 1, L_SUM).wait_send()
    side_l.wait_send()
    batch(gwz, Z - 1, W_LEVEL).wait_send()
    put_r.wait()
    put_l.wait()
    put_w.wait()


def body(left_act, right_act, cotangent, weight):
    vm = pltpu.VMEM
    dma = pltpu.SemaphoreType.DMA
    msg = (32, 128)
    return pl.pallas_call(
        kernel,
        out_shape=[
            jax.ShapeDtypeStruct(left_act.shape, F32),
            jax.ShapeDtypeStruct(right_act.shape, F32),
            jax.ShapeDtypeStruct(msg, F32),
        ],
        in_specs=[pl.BlockSpec(memory_space=pltpu.HBM)] * 4,
        out_specs=[pl.BlockSpec(memory_space=pltpu.HBM)] * 3,
        scratch_shapes=[
            vm((C, 4, 32), BF), vm((C, 2, 64), BF), vm((2048, 128), BF), vm((1024, 128), BF),
            vm((64, 128), F32), vm((128, 128), F32), vm(msg, F32), vm(msg, BF), vm(msg, BF),
            vm((2, Q, *msg), BF), vm((16, *msg), BF),
            vm((1024, 128), F32), vm((512, 128), F32), vm((1024, 128), F32), vm((1024, 128), BF),
            vm((128, 512), BF), vm((512, 128), BF), vm((16, 128, 256), BF),
            vm((16, C, C, 128), BF), vm((16, C, C, 128), BF),
            vm((C, C, 128), F32), vm((C, Q, 128), F32), vm((512, 128), F32),
            vm((Q, *msg), BF), vm((Q, *msg), BF), vm((Z, *msg), BF), vm(msg, BF), vm(msg, F32), vm(msg, F32),
            vm((16, S, 128), F32), vm((16, 32, 128), F32), vm((512, 128), F32),
            vm((Q, *msg), BF), vm((Q, *msg), BF), vm((2, *msg), F32),
            vm((4, 128, 128), F32), vm((Z, 2, *msg), BF), vm((Z, 2, *msg), BF), vm(msg, F32), vm(msg, F32),
            vm(msg, F32), vm((128, 128), F32), vm((128, 128), F32),
            vm(msg, F32), vm((C, 2, 64), F32), vm((C, 4, 32), F32), dma((4,)), dma((3,)), dma((12,)), dma((12,)),
        ],
        compiler_params=pltpu.CompilerParams(
            collective_id=0, has_side_effects=True
        ),
    )(left_act, right_act, cotangent.reshape(2048, 128), weight)


def solution(mesh):
    return jax.shard_map(
        body,
        mesh=mesh,
        in_specs=(P(None, "col", "row"), P(None, "row", "col"), P("row", "col", None), P()),
        out_specs=(P(None, "col", "row"), P(None, "row", "col"), P("row", None)),
        check_vma=False,
    )
```

time: 55.8 us -> 47.1 us (0.84)
  the two profiles are of different devices: /device:TPU:14 before, /device:TPU:1 now
where the time goes in v2:
time: 47.1 us; the launch traced here: 46.8 us
  Pallas kernels  43.3 us (92%)
  local copies, waits for them, and re-layouts  2.82 us (6%)
  between operations  0.65 us (1%)
    pallas_call x1, Pallas kernels, body(): pl.pallas_call(kernel, out_shape=[jax.ShapeDtypeStruct(left_act.shape, F3...  43.3 us
    unnamed x7, local copies, waits for them, and re-layouts  2.82 us

profile of v2, /device:TPU:1, one launch (start us, length us, event | category | flops | bytes accessed | tf_op | source)
XLA Modules:
  0.0 46.8 jit_solution(3759222584609957030)
XLA Ops:
  0.6 43.3 %shard_map.67 = (f32[32,4,32]{2,1,0:T(4,128)}, f32[32,2,64]{2,1,0:T(2,128)}, f32[32,128]{1,0:T(8,128)}) custom-call(bf16[32,4,32]{2,1,0:T(4,128)(2,1)} %l_in.1, bf16[32,2,64]{2,1,0:T(2,128)(2,1)} %r_in.1, bf16[2048,128]{1,0:T(8,128)(2,1)} %bitcast.1, bf16[1024,128]{1,0:T(8,128)(2,1)} %w_in.1), custom_call_target="tpu_custom_call" | custom-call | tf_op jit(solution)/shard_map/pallas_call | solution.py:353
  44.0 0.0 copy-start
  44.0 1.5 %copy.10 = f32[32,4,32]{2,1,0:T(4,128)} copy(f32[32,4,32]{2,1,0:T(4,128)} %get-tuple-element.6) | data formatting | bytes 32768
  45.5 0.0 copy-done
  45.5 0.0 copy-start.1
  45.5 0.6 %copy.11 = f32[32,2,64]{2,1,0:T(2,128)} copy(f32[32,2,64]{2,1,0:T(2,128)S(1)} %copy-done) | data formatting | bytes 32768
  46.1 0.1 copy-done.1
  46.2 0.6 %copy.12 = f32[32,128]{1,0:T(8,128)} copy(f32[32,128]{1,0:T(8,128)S(1)} %copy-done.1) | data formatting | bytes 32768
Async XLA Ops:
  44.0 1.5 %copy-start = (f32[32,2,64]{2,1,0:T(2,128)S(1)}, f32[32,2,64]{2,1,0:T(2,128)}, u32[]{:S(2)}) copy-start(f32[32,2,64]{2,1,0:T(2,128)} %get-tuple-element.7) | copy-start | bytes 49156
  45.5 0.7 %copy-start.1 = (f32[32,128]{1,0:T(8,128)S(1)}, f32[32,128]{1,0:T(8,128)}, u32[]{:S(2)}) copy-start(f32[32,128]{1,0:T(8,128)} %get-tuple-element.8) | copy-start | bytes 49156

commit v3 on v2

--- a/solution.py
+++ b/solution.py
@@ -12,7 +12,7 @@
 C = 32
 Q = 16
 Z = 8
-R_ROW, R_PAIR, L_SIDE, L_LEVEL, W_PAIR, W_ROW, W_LEVEL, G_PAIR, G_ROW, L_SUM, L_SUM_SIDE, W_SIDE = range(12)
+R_ROW, R_PAIR, L_SIDE, L_LEVEL, W_X, W_Y, W_LEVEL, G_PAIR, G_ROW, L_SUM, L_SUM_SIDE = range(11)
 
 
 def dot(a, b, dims=((1,), (0,))):
@@ -36,7 +36,7 @@
     gl_out, gr_out, gw_out,
     lv, rv, g, w, ra, la, lb, rmsg, lmsg,
     rbuf, lbuf, fr, fl, wf, wp, lt, l2, bd, xb, yb,
-    gws, gwp, gwh, gwsend, gwrecv, gwz, gwzs, gwy, gwys,
+    gws, gwsend, gwx, gwysend, gwy, gwz, gwzs,
     grs, grp, grh, grsend, grrecv, grf,
     gls, glsend, glrecv, gly, glys, glf, gt, ga,
     gwo, gro, glo, in_sem, out_sem, sent, got,
@@ -44,6 +44,7 @@
     row, col = lax.axis_index("row"), lax.axis_index("col")
     core, q = lax.rem(row, 2), row // 2
     yh, z = lax.rem(col, 2), col // 2
+    me_x, me_y = lax.rem(row, 8), 4 * yh + row // 8
     pair = (row + 1 - 2 * core, col)
     other = (row, col + 1 - 2 * yh)
 
@@ -202,14 +203,24 @@
             b = xb[2 * p + 1, pl.ds(n * 8, 8)].reshape(256, 128)
             term = dot(jnp.concatenate([a, b], axis=1), g[p * 256 : (p + 1) * 256, :])
             total = term if total is None else total + term
-        gws[pl.ds(n * 8, 8)] = total.reshape(8, C, 128)
+        gws[pl.ds(pl.multiple_of(n * 256, 256), 256), :] = total
 
     for t in range(16):
         outer(t)
     for n in range(4):
         grad_w(n)
-    w_pair = remote(gws.at[:, pl.ds(pl.multiple_of((1 - core) * Q, Q), Q), :], gwp, W_PAIR, pair)
-    w_pair.start()
+    def fill_w(m):
+        for n in range(4):
+            gwsend[m, n] = gws[pl.ds(lax.rem(m, 2) * Q + n * 4 + m // 2, 32, stride=C), :].astype(BF)
+
+    def x_mate(k):
+        return lax.rem(me_x + k, 8)
+
+    each(0, 4, some(2, fill_w))
+    each(
+        1, 8,
+        lambda k: remote(gwsend.at[x_mate(k)], gwx.at[me_x], W_X, (row - me_x + x_mate(k), col)).start(),
+    )
 
     def grad_r(t):
         y = jnp.concatenate([yb[:, 2 * t].reshape(512, 128), yb[:, 2 * t + 1].reshape(512, 128)], axis=1)
@@ -218,16 +229,7 @@
         c, d = x[:S, 128:], x[S:, 128:]
         grs[t] = jnp.where(low, a, d) + pltpu.roll(jnp.where(low, c, b), 64, 1)
 
-    each(0, 2, some(4, grad_r))
-    w_pair.wait_recv()
-    gwh[...] = (gws[:, pl.ds(pl.multiple_of(core * Q, Q), Q), :] + gwp[...]).reshape(512, 128)
-
-    def fill_w(k):
-        gwsend[k] = gwh[pl.ds(k, 32, stride=Q), :].astype(BF)
-
-    each(0, 2, some(8, fill_w))
-    each(1, Q, lambda k: remote(gwsend.at[chip(k)], gwrecv.at[q], W_ROW, row_mate(k)).start())
-    each(2, 4, some(4, grad_r))
+    each(0, 4, some(4, grad_r))
 
     g_pair = remote(grs.at[:, pl.ds(pl.multiple_of((1 - core) * 32, 32), 32), :], grp, G_PAIR, pair)
     g_pair.start()
@@ -256,7 +258,6 @@
         grsend[chip(k)] = grh[pl.ds(chip(k), 32, stride=Q), :].astype(BF)
 
     each(0, 4, some(4, fill_g))
-    each(1, Q, lambda k: remote(grsend.at[chip(k)], grrecv.at[q], G_ROW, row_mate(k)).start())
 
     def l_rows(c):
         return jnp.concatenate([gls[tile, pl.ds(c, 8, stride=Q), :] for tile in range(4)], axis=0)
@@ -269,13 +270,26 @@
 
     each(1, Z, lambda k: remote(glsend.at[level(k)], glrecv.at[z], L_SUM, z_mate(k)).start())
 
-    batch(gwrecv, Q - 1, W_ROW).wait_recv()
-    acc = gwh[pl.ds(q, 32, stride=Q), :]
-    for k in range(1, Q):
-        acc = acc + gwrecv[chip(k)].astype(F32)
-    total_w = acc.astype(BF)
-    gwzs[...] = total_w
-    gwz[z] = total_w
+    batch(gwx, 7, W_X).wait_recv()
+    for n in range(4):
+        acc = gws[pl.ds(core * Q + n * 4 + me_x // 2, 32, stride=C), :]
+        for k in range(1, 8):
+            acc = acc + gwx[x_mate(k), n].astype(F32)
+        gwysend[n] = acc.astype(BF)
+
+    def y_mate(k):
+        there = lax.rem(me_y + k, 8)
+        return lax.rem(there, 4), (lax.rem(there, 4) * 8 + me_x, 2 * z + there // 4)
+
+    each(1, 8, lambda k: remote(gwysend.at[y_mate(k)[0]], gwy.at[me_y], W_Y, y_mate(k)[1]).start())
+    each(1, Q, lambda k: remote(grsend.at[chip(k)], grrecv.at[q], G_ROW, row_mate(k)).start())
+    gwy[me_y] = gwysend[lax.rem(me_y, 4)]
+    batch(gwy, 7, W_Y).wait_recv()
+    acc = gwy[0].astype(F32)
+    for n in range(1, 8):
+        acc = acc + gwy[n].astype(F32)
+    gwzs[...] = acc
+    gwz[z] = acc
     each(1, Z, lambda k: remote(gwzs, gwz.at[z], W_LEVEL, z_mate(k)).start())
 
     batch(glrecv, Z - 1, L_SUM).wait_recv()
@@ -305,13 +319,6 @@
     put_r.start()
 
     gt[...] = jnp.zeros_like(gt)
-    batch(gwz, Z - 1, W_LEVEL).wait_recv()
-    acc = gwz[0].astype(F32)
-    for n in range(1, Z):
-        acc = acc + gwz[n].astype(F32)
-    gwys[...] = acc
-    side_w = remote(gwys, gwy, W_SIDE, other)
-    side_w.start()
     side_l.wait_recv()
     glf[...] = (glf[...] + gly[...]) * (1.0 / S)
     parts = swap_groups([glf[pl.ds(s, 8, stride=4), :] for s in range(4)], group)
@@ -324,8 +331,11 @@
     put_l = pltpu.make_async_copy(glo, gl_out, out_sem.at[1])
     put_l.start()
 
-    side_w.wait_recv()
-    gwo[...] = gwys[...] + gwy[...]
+    batch(gwz, Z - 1, W_LEVEL).wait_recv()
+    acc = gwz[0]
+    for n in range(1, Z):
+        acc = acc + gwz[n]
+    gwo[...] = acc
     put_w = pltpu.make_async_copy(gwo, gw_out, out_sem.at[2])
     put_w.start()
 
@@ -333,9 +343,8 @@
     l_side.wait_send()
     batch(lbuf, 2 * (Z - 1), L_LEVEL).wait_send()
     r_pair.wait_send()
-    w_pair.wait_send()
-    batch(gwrecv, Q - 1, W_ROW).wait_send()
-    side_w.wait_send()
+    batch(gwsend, 7, W_X).wait_send()
+    batch(gwy, 7, W_Y).wait_send()
     g_pair.wait_send()
     batch(grsend, Q - 1, G_ROW).wait_send()
     batch(glsend, Z - 1, L_SUM).wait_send()
@@ -346,11 +355,24 @@
     put_w.wait()
 
 
+def put(a_in, b_in, c_in, a_out, b_out, c_out, a, b, c, in_sem, out_sem):
+    sides = [(a_in, a, a_out), (b_in, b, b_out), (c_in, c, c_out)]
+    reads = [pltpu.make_async_copy(src, mid, in_sem.at[n]) for n, (src, mid, _) in enumerate(sides)]
+    writes = [pltpu.make_async_copy(mid, dst, out_sem.at[n]) for n, (_, mid, dst) in enumerate(sides)]
+    for read in reads:
+        read.start()
+    for read, write in zip(reads, writes):
+        read.wait()
+        write.start()
+    for write in writes:
+        write.wait()
+
+
 def body(left_act, right_act, cotangent, weight):
     vm = pltpu.VMEM
     dma = pltpu.SemaphoreType.DMA
     msg = (32, 128)
-    return pl.pallas_call(
+    parts = pl.pallas_call(
         kernel,
         out_shape=[
             jax.ShapeDtypeStruct(left_act.shape, F32),
@@ -366,18 +388,26 @@
             vm((1024, 128), F32), vm((512, 128), F32), vm((1024, 128), F32), vm((1024, 128), BF),
             vm((128, 512), BF), vm((512, 128), BF), vm((16, 128, 256), BF),
             vm((16, C, C, 128), BF), vm((16, C, C, 128), BF),
-            vm((C, C, 128), F32), vm((C, Q, 128), F32), vm((512, 128), F32),
-            vm((Q, *msg), BF), vm((Q, *msg), BF), vm((Z, *msg), BF), vm(msg, BF), vm(msg, F32), vm(msg, F32),
+            vm((1024, 128), F32), vm((8, 4, *msg), BF), vm((8, 4, *msg), BF),
+            vm((4, *msg), BF), vm((8, *msg), BF), vm((Z, *msg), F32), vm(msg, F32),
             vm((16, S, 128), F32), vm((16, 32, 128), F32), vm((512, 128), F32),
             vm((Q, *msg), BF), vm((Q, *msg), BF), vm((2, *msg), F32),
             vm((4, 128, 128), F32), vm((Z, 2, *msg), BF), vm((Z, 2, *msg), BF), vm(msg, F32), vm(msg, F32),
             vm(msg, F32), vm((128, 128), F32), vm((128, 128), F32),
-            vm(msg, F32), vm((C, 2, 64), F32), vm((C, 4, 32), F32), dma((4,)), dma((3,)), dma((12,)), dma((12,)),
+            vm(msg, F32), vm((C, 2, 64), F32), vm((C, 4, 32), F32), dma((4,)), dma((3,)), dma((11,)), dma((11,)),
         ],
         compiler_params=pltpu.CompilerParams(
             collective_id=0, has_side_effects=True
         ),
     )(left_act, right_act, cotangent.reshape(2048, 128), weight)
+    shapes = [part.shape for part in parts]
+    return pl.pallas_call(
+        put,
+        out_shape=[jax.ShapeDtypeStruct(shape, F32) for shape in shapes],
+        in_specs=[pl.BlockSpec(memory_space=pl.ANY)] * 3,
+        out_specs=[pl.BlockSpec(memory_space=pl.ANY)] * 3,
+        scratch_shapes=[*(vm(shape, F32) for shape in shapes), dma((3,)), dma((3,))],
+    )(*parts)
 
 
 def solution(mesh):

time: 47.1 us -> 44.8 us (0.951)
  local copies, waits for them, and re-layouts: 2.82 us -> 0 us
  Pallas kernels: 43.3 us -> 44 us
    unnamed x7 -> x0, local copies, waits for them, and re-layouts: 2.82 us -> none
    pallas_call x0 -> x1, Pallas kernels: none -> 1.53 us  [body(): pl.pallas_call(put, out_shape=[jax.ShapeDtypeStruct(shape, F32) for shape...]
    pallas_call x1, Pallas kernels: 43.3 us -> 42.5 us  [body(): pl.pallas_call(kernel, out_shape=[jax.ShapeDtypeStruct(left_act.shape, F3...]
where the time goes in v3:
time: 44.8 us; the launch traced here: 44.6 us
  Pallas kernels  44 us (98%)
  between operations  0.64 us (1%)
    pallas_call x1, Pallas kernels, body(): pl.pallas_call(kernel, out_shape=[jax.ShapeDtypeStruct(left_act.shape, F3...  42.5 us
    pallas_call x1, Pallas kernels, body(): pl.pallas_call(put, out_shape=[jax.ShapeDtypeStruct(shape, F32) for shape...  1.53 us

profile of v3, /device:TPU:1, one launch (start us, length us, event | category | flops | bytes accessed | tf_op | source)
XLA Modules:
  0.0 44.6 jit_solution(1588949211479848853)
XLA Ops:
  0.6 42.5 %shard_map.67 = (f32[32,4,32]{2,1,0:T(4,128)}, f32[32,2,64]{2,1,0:T(2,128)}, f32[32,128]{1,0:T(8,128)}) custom-call(bf16[32,4,32]{2,1,0:T(4,128)(2,1)} %l_in.1, bf16[32,2,64]{2,1,0:T(2,128)(2,1)} %r_in.1, bf16[2048,128]{1,0:T(8,128)(2,1)} %bitcast.1, bf16[1024,128]{1,0:T(8,128)(2,1)} %w_in.1), custom_call_target="tpu_custom_call" | custom-call | tf_op jit(solution)/shard_map/pallas_call | solution.py:375
  43.1 1.5 %shard_map.68 = (f32[32,4,32]{2,1,0:T(4,128)}, f32[32,2,64]{2,1,0:T(2,128)}, f32[32,128]{1,0:T(8,128)}) custom-call(f32[32,4,32]{2,1,0:T(4,128)} %get-tuple-element.6.a_in, f32[32,2,64]{2,1,0:T(2,128)} %get-tuple-element.7.b_in, f32[32,128]{1,0:T(8,128)} %get-tuple-element.8.c_in), custom_call_target="tpu_custom_call" | custom-call | tf_op jit(solution)/shard_map/pallas_call | solution.py:404

commit v4 on v3

--- a/solution.py
+++ b/solution.py
@@ -12,6 +12,7 @@
 C = 32
 Q = 16
 Z = 8
+FAR_FIRST = (4, 3, 5, 2, 6, 1, 7)
 R_ROW, R_PAIR, L_SIDE, L_LEVEL, W_X, W_Y, W_LEVEL, G_PAIR, G_ROW, L_SUM, L_SUM_SIDE = range(11)
 
 
@@ -39,7 +40,7 @@
     gws, gwsend, gwx, gwysend, gwy, gwz, gwzs,
     grs, grp, grh, grsend, grrecv, grf,
     gls, glsend, glrecv, gly, glys, glf, gt, ga,
-    gwo, gro, glo, in_sem, out_sem, sent, got,
+    in_sem, sent, got,
 ):
     row, col = lax.axis_index("row"), lax.axis_index("col")
     core, q = lax.rem(row, 2), row // 2
@@ -82,9 +83,10 @@
     def greet(device):
         pl.semaphore_signal(barrier, inc=1, device_id=device, device_id_type=MESH)
 
+    greet(other)
+    for k in FAR_FIRST:
+        greet(z_mate(k))
     each(1, Q, lambda k: greet(row_mate(k)))
-    greet(other)
-    each(1, Z, lambda k: greet(z_mate(k)))
     greet(pair)
 
     copies = [
@@ -126,7 +128,8 @@
     side_col = col + 1 - 2 * yh
     l_side = remote(lmsg, lbuf.at[col], L_SIDE, other)
     l_side.start()
-    each(1, Z, lambda k: remote(lmsg, lbuf.at[col], L_LEVEL, z_mate(k)).start())
+    for k in FAR_FIRST:
+        remote(lmsg, lbuf.at[col], L_LEVEL, z_mate(k)).start()
     r_slots = rbuf.at[core]
     each(1, Q, lambda k: remote(rmsg, r_slots.at[q], R_ROW, row_mate(k)).start())
 
@@ -158,7 +161,8 @@
 
     l_side.wait_recv()
     forward = lbuf.at[side_col]
-    each(1, Z, lambda k: remote(forward, forward, L_LEVEL, z_mate(k)).start())
+    for k in FAR_FIRST:
+        remote(forward, forward, L_LEVEL, z_mate(k)).start()
 
     batch(r_slots, Q - 1, R_ROW).wait_recv()
     r_pair = remote(r_slots, r_slots, R_PAIR, pair)
@@ -217,10 +221,8 @@
         return lax.rem(me_x + k, 8)
 
     each(0, 4, some(2, fill_w))
-    each(
-        1, 8,
-        lambda k: remote(gwsend.at[x_mate(k)], gwx.at[me_x], W_X, (row - me_x + x_mate(k), col)).start(),
-    )
+    for k in FAR_FIRST:
+        remote(gwsend.at[x_mate(k)], gwx.at[me_x], W_X, (row - me_x + x_mate(k), col)).start()
 
     def grad_r(t):
         y = jnp.concatenate([yb[:, 2 * t].reshape(512, 128), yb[:, 2 * t + 1].reshape(512, 128)], axis=1)
@@ -281,7 +283,9 @@
         there = lax.rem(me_y + k, 8)
         return lax.rem(there, 4), (lax.rem(there, 4) * 8 + me_x, 2 * z + there // 4)
 
-    each(1, 8, lambda k: remote(gwysend.at[y_mate(k)[0]], gwy.at[me_y], W_Y, y_mate(k)[1]).start())
+    for k in FAR_FIRST:
+        part, mate = y_mate(k)
+        remote(gwysend.at[part], gwy.at[me_y], W_Y, mate).start()
     each(1, Q, lambda k: remote(grsend.at[chip(k)], grrecv.at[q], G_ROW, row_mate(k)).start())
     gwy[me_y] = gwysend[lax.rem(me_y, 4)]
     batch(gwy, 7, W_Y).wait_recv()
@@ -290,7 +294,8 @@
         acc = acc + gwy[n].astype(F32)
     gwzs[...] = acc
     gwz[z] = acc
-    each(1, Z, lambda k: remote(gwzs, gwz.at[z], W_LEVEL, z_mate(k)).start())
+    for k in FAR_FIRST:
+        remote(gwzs, gwz.at[z], W_LEVEL, z_mate(k)).start()
 
     batch(glrecv, Z - 1, L_SUM).wait_recv()
 
@@ -314,9 +319,7 @@
     grf[1] = pltpu.roll(acc_r, 64, 1)
     for t in range(16):
         for dd in range(2):
-            gro[2 * t + dd] = grf[dd, 2 * t : 2 * t + 2, :64]
-    put_r = pltpu.make_async_copy(gro, gr_out, out_sem.at[0])
-    put_r.start()
+            gr_out[2 * t + dd] = grf[dd, 2 * t : 2 * t + 2, :64]
 
     gt[...] = jnp.zeros_like(gt)
     side_l.wait_recv()
@@ -327,17 +330,13 @@
             gt[tile * 8 + 2 * a : tile * 8 + 2 * a + 2, :] = parts[a][2 * tile : 2 * tile + 2]
     ga[...] = gt[...].T
     for c in range(C):
-        glo[c] = ga[pl.ds(c % 2 * Q + c // 2, 4, stride=32), :][:, :32]
-    put_l = pltpu.make_async_copy(glo, gl_out, out_sem.at[1])
-    put_l.start()
+        gl_out[c] = ga[pl.ds(c % 2 * Q + c // 2, 4, stride=32), :][:, :32]
 
     batch(gwz, Z - 1, W_LEVEL).wait_recv()
     acc = gwz[0]
     for n in range(1, Z):
         acc = acc + gwz[n]
-    gwo[...] = acc
-    put_w = pltpu.make_async_copy(gwo, gw_out, out_sem.at[2])
-    put_w.start()
+    gw_out[...] = acc
 
     batch(r_slots, Q - 1, R_ROW).wait_send()
     l_side.wait_send()
@@ -350,19 +349,12 @@
     batch(glsend, Z - 1, L_SUM).wait_send()
     side_l.wait_send()
     batch(gwz, Z - 1, W_LEVEL).wait_send()
-    put_r.wait()
-    put_l.wait()
-    put_w.wait()
-
-
-def put(a_in, b_in, c_in, a_out, b_out, c_out, a, b, c, in_sem, out_sem):
-    sides = [(a_in, a, a_out), (b_in, b, b_out), (c_in, c, c_out)]
-    reads = [pltpu.make_async_copy(src, mid, in_sem.at[n]) for n, (src, mid, _) in enumerate(sides)]
-    writes = [pltpu.make_async_copy(mid, dst, out_sem.at[n]) for n, (_, mid, dst) in enumerate(sides)]
-    for read in reads:
-        read.start()
-    for read, write in zip(reads, writes):
-        read.wait()
+
+
+def put(a_in, b_in, c_in, a_out, b_out, c_out, sem):
+    sides = [(a_in, a_out), (b_in, b_out), (c_in, c_out)]
+    writes = [pltpu.make_async_copy(src, dst, sem.at[n]) for n, (src, dst) in enumerate(sides)]
+    for write in writes:
         write.start()
     for write in writes:
         write.wait()
@@ -380,7 +372,7 @@
             jax.ShapeDtypeStruct(msg, F32),
         ],
         in_specs=[pl.BlockSpec(memory_space=pltpu.HBM)] * 4,
-        out_specs=[pl.BlockSpec(memory_space=pltpu.HBM)] * 3,
+        out_specs=[pl.BlockSpec(memory_space=vm)] * 3,
         scratch_shapes=[
             vm((C, 4, 32), BF), vm((C, 2, 64), BF), vm((2048, 128), BF), vm((1024, 128), BF),
             vm((64, 128), F32), vm((128, 128), F32), vm(msg, F32), vm(msg, BF), vm(msg, BF),
@@ -394,19 +386,22 @@
             vm((Q, *msg), BF), vm((Q, *msg), BF), vm((2, *msg), F32),
             vm((4, 128, 128), F32), vm((Z, 2, *msg), BF), vm((Z, 2, *msg), BF), vm(msg, F32), vm(msg, F32),
             vm(msg, F32), vm((128, 128), F32), vm((128, 128), F32),
-            vm(msg, F32), vm((C, 2, 64), F32), vm((C, 4, 32), F32), dma((4,)), dma((3,)), dma((11,)), dma((11,)),
+            dma((4,)), dma((11,)), dma((11,)),
         ],
         compiler_params=pltpu.CompilerParams(
-            collective_id=0, has_side_effects=True
+            collective_id=0, has_side_effects=True, vmem_limit_bytes=32 * 1024 * 1024
         ),
-    )(left_act, right_act, cotangent.reshape(2048, 128), weight)
+    )(
+        *(pltpu.with_memory_space_constraint(a, pltpu.HBM) for a in (left_act, right_act, cotangent.reshape(2048, 128), weight))
+    )
     shapes = [part.shape for part in parts]
     return pl.pallas_call(
         put,
         out_shape=[jax.ShapeDtypeStruct(shape, F32) for shape in shapes],
-        in_specs=[pl.BlockSpec(memory_space=pl.ANY)] * 3,
+        in_specs=[pl.BlockSpec(memory_space=vm)] * 3,
         out_specs=[pl.BlockSpec(memory_space=pl.ANY)] * 3,
-        scratch_shapes=[*(vm(shape, F32) for shape in shapes), dma((3,)), dma((3,))],
+        scratch_shapes=[dma((3,))],
+        compiler_params=pltpu.CompilerParams(vmem_limit_bytes=2097152),
     )(*parts)
 
 

time: 44.8 us -> 42.6 us (0.951)
  the two profiles are of different devices: /device:TPU:1 before, /device:TPU:8 now
where the time goes in v4:
time: 42.6 us; the launch traced here: 42.5 us
  Pallas kernels  41.8 us (98%)
  between operations  0.64 us (2%)
    pallas_call x1, Pallas kernels, body(): pl.pallas_call(kernel, out_shape=[jax.ShapeDtypeStruct(left_act.shape, F3...  41.2 us

profile of v4, /device:TPU:8, one launch (start us, length us, event | category | flops | bytes accessed | tf_op | source)
XLA Modules:
  0.0 42.5 jit_solution(9693223348502817396)
XLA Ops:
  0.6 41.2 %shard_map.67 = (f32[32,4,32]{2,1,0:T(4,128)S(1)}, f32[32,2,64]{2,1,0:T(2,128)S(1)}, f32[32,128]{1,0:T(8,128)S(1)}) custom-call(bf16[32,4,32]{2,1,0:T(4,128)(2,1)} %l_in.1, bf16[32,2,64]{2,1,0:T(2,128)(2,1)} %r_in.1, bf16[2048,128]{1,0:T(8,128)(2,1)} %bitcast.1, bf16[1024,128]{1,0:T(8,128)(2,1)} %w_in.1), custom_call_target="tpu_custom_call" | custom-call | tf_op jit(solution)/shard_map/pallas_call | solution.py:367
  41.8 0.7 %shard_map.68 = (f32[32,4,32]{2,1,0:T(4,128)}, f32[32,2,64]{2,1,0:T(2,128)}, f32[32,128]{1,0:T(8,128)}) custom-call(f32[32,4,32]{2,1,0:T(4,128)S(1)} %get-tuple-element.6.a_in, f32[32,2,64]{2,1,0:T(2,128)S(1)} %get-tuple-element.7.b_in, f32[32,128]{1,0:T(8,128)S(1)} %get-tuple-element.8.c_in), custom_call_target="tpu_custom_call" | custom-call | tf_op jit(solution)/shard_map/pallas_call | solution.py:398

commit v5 on v4

--- a/solution.py
+++ b/solution.py
@@ -128,10 +128,10 @@
     side_col = col + 1 - 2 * yh
     l_side = remote(lmsg, lbuf.at[col], L_SIDE, other)
     l_side.start()
-    for k in FAR_FIRST:
-        remote(lmsg, lbuf.at[col], L_LEVEL, z_mate(k)).start()
     r_slots = rbuf.at[core]
     each(1, Q, lambda k: remote(rmsg, r_slots.at[q], R_ROW, row_mate(k)).start())
+    for k in FAR_FIRST:
+        remote(lmsg, lbuf.at[col], L_LEVEL, z_mate(k)).start()
 
     copies[2].wait()
     wf[...] = w[...].astype(F32)
@@ -270,7 +270,8 @@
 
     each(0, 2, some(4, fill_l))
 
-    each(1, Z, lambda k: remote(glsend.at[level(k)], glrecv.at[z], L_SUM, z_mate(k)).start())
+    for k in FAR_FIRST:
+        remote(glsend.at[level(k)], glrecv.at[z], L_SUM, z_mate(k)).start()
 
     batch(gwx, 7, W_X).wait_recv()
     for n in range(4):

time: 42.6 us -> 42.5 us (level)
  no operation moved by 1% of the time
where the time goes in v5:
time: 42.5 us; the launch traced here: 42.3 us
  Pallas kernels  41.7 us (98%)
  between operations  0.64 us (2%)
    pallas_call x1, Pallas kernels, body(): pl.pallas_call(kernel, out_shape=[jax.ShapeDtypeStruct(left_act.shape, F3...  41 us

profile of v5, /device:TPU:8, one launch (start us, length us, event | category | flops | bytes accessed | tf_op | source)
XLA Modules:
  0.0 42.3 jit_solution(89325586660214738)
XLA Ops:
  0.6 41.0 %shard_map.67 = (f32[32,4,32]{2,1,0:T(4,128)S(1)}, f32[32,2,64]{2,1,0:T(2,128)S(1)}, f32[32,128]{1,0:T(8,128)S(1)}) custom-call(bf16[32,4,32]{2,1,0:T(4,128)(2,1)} %l_in.1, bf16[32,2,64]{2,1,0:T(2,128)(2,1)} %r_in.1, bf16[2048,128]{1,0:T(8,128)(2,1)} %bitcast.1, bf16[1024,128]{1,0:T(8,128)(2,1)} %w_in.1), custom_call_target="tpu_custom_call" | custom-call | tf_op jit(solution)/shard_map/pallas_call | solution.py:368
  41.7 0.7 %shard_map.68 = (f32[32,4,32]{2,1,0:T(4,128)}, f32[32,2,64]{2,1,0:T(2,128)}, f32[32,128]{1,0:T(8,128)}) custom-call(f32[32,4,32]{2,1,0:T(4,128)S(1)} %get-tuple-element.6.a_in, f32[32,2,64]{2,1,0:T(2,128)S(1)} %get-tuple-element.7.b_in, f32[32,128]{1,0:T(8,128)S(1)} %get-tuple-element.8.c_in), custom_call_target="tpu_custom_call" | custom-call | tf_op jit(solution)/shard_map/pallas_call | solution.py:399
